TPU v7x, 32 devices: a whole 2x2x4 slice. The times are simulated.
32 devices in a mesh: blk: 2 (over core), dp: 16 (over z, y, x).
Axes of the slice: x: 2, y: 2, z: 4, core: 2. Of those that a mesh axis runs over, the one named last changes fastest.
Arguments:
- queries: bfloat16 [4096, 256], P(('blk', 'dp')), may hold values from -1 to 1, as said below
- items: bfloat16 [4096, 256], P(('blk', 'dp')), may hold values from -1 to 1, as said below
Outputs:
- loss: float32 [], replicated
- question_slope: float32 [4096, 256], P(('blk', 'dp'))
- candidate_slope: float32 [4096, 256], P(('blk', 'dp'))
Inputs may be any that keep to these rules, and one draw needn't show every extreme that they name: queries: entries lie between -1 and 1 and no row is zero; each query is close to its own item and to one item of the batch chosen by a random permutation (which may be its own). items: entries lie between -1 and 1 and no row is zero.
All inputs are finite; a program needn't handle non-finite values.
Results may differ from a plain program's by a relative error of at most 0.008.
Values may be sent and summed in bfloat16 or wider, within the bound.
A program may use at most 64 MiB of HBM per device.

v0:
```python
import math

import jax
import jax.numpy as jnp
from jax import lax
from jax.sharding import PartitionSpec as P

softmax_sharpness = 0.05
tiny_square = 1e-12


def taken_in(shard, axis, dim, absorb, state):
    everything = jax.tree.map(lambda a: lax.all_gather(a, axis, axis=dim, tiled=True), shard)
    return absorb(state, everything, jnp.int32(0))


def unit_rows(matrix):
    widened = matrix.astype(jnp.float32)
    length = jnp.sqrt(jnp.sum(widened * widened, axis=1, keepdims=True) + tiny_square)
    return (widened / length, length)


def direction_slope(grad, unit, length):
    along = jnp.sum(unit * grad, axis=1, keepdims=True)
    return (grad - unit * along) / length


def split_rows(matrix, step_rows):
    return matrix.reshape((matrix.shape[0] // step_rows, step_rows) + matrix.shape[1:])


def per_device(queries, items):
    question_direction, question_magnitude = unit_rows(queries)
    candidate_direction, candidate_magnitude = unit_rows(items)
    normalized_question = question_direction.astype(jnp.bfloat16)
    normalized_candidate = candidate_direction.astype(jnp.bfloat16)
    question_gathered_all = normalized_question.astype(jnp.float32)
    candidate_gathered_all = normalized_candidate.astype(jnp.float32)
    own_rows = normalized_question.shape[0]
    matching_score = (
        jnp.sum(question_gathered_all * candidate_gathered_all, axis=1) / softmax_sharpness
    )

    def norm_step(running, shard_rows, first_row):
        step_rows = math.gcd(shard_rows.shape[0], 512)

        def per_block(state, candidate_slice):
            old_peak, old_total = state
            similarity_scores = (
                jnp.dot(normalized_question, candidate_slice.T, preferred_element_type=jnp.float32)
                / softmax_sharpness
            )
            new_peak = jnp.maximum(old_peak, jnp.max(similarity_scores, axis=1))
            new_total = old_total * jnp.exp(old_peak - new_peak) + jnp.sum(
                jnp.exp(similarity_scores - new_peak[:, None]), axis=1
            )
            return ((new_peak, new_total), None)

        result, _ = lax.scan(per_block, running, split_rows(shard_rows, step_rows))
        return result

    start_state = (jnp.full((own_rows,), -1e30, jnp.float32), jnp.zeros((own_rows,), jnp.float32))
    peak, summed = taken_in(normalized_candidate, ("blk", "dp"), 0, norm_step, start_state)
    log_norm = peak + jnp.log(summed)
    local_loss = jnp.sum(log_norm - matching_score)
    devices = lax.axis_size(("blk", "dp"))
    loss = lax.psum(local_loss, ("blk", "dp")) / (own_rows * devices)
    empty_grad = jnp.zeros(normalized_question.shape, jnp.float32)

    def query_step(running, shard_rows, first_row):
        step_rows = math.gcd(shard_rows.shape[0], 512)

        def per_block(acc_grad, candidate_slice):
            similarity_scores = (
                jnp.dot(normalized_question, candidate_slice.T, preferred_element_type=jnp.float32)
                / softmax_sharpness
            )
            weights = jnp.exp(similarity_scores - log_norm[:, None]).astype(jnp.bfloat16)
            return (
                acc_grad + jnp.dot(weights, candidate_slice, preferred_element_type=jnp.float32),
                None,
            )

        result, _ = lax.scan(per_block, running, split_rows(shard_rows, step_rows))
        return result

    question_count_overall = taken_in(
        normalized_candidate, ("blk", "dp"), 0, query_step, empty_grad
    )

    def item_step(running, shard_rows, first_row):
        q_rows, q_norms = shard_rows
        step_rows = math.gcd(q_rows.shape[0], 512)

        def per_block(acc_grad, pieces):
            question_portion, norm_part = pieces
            question_slice_local = question_portion.astype(jnp.bfloat16)
            similarity_scores = (
                jnp.dot(
                    question_slice_local, normalized_candidate.T, preferred_element_type=jnp.float32
                )
                / softmax_sharpness
            )
            weights = jnp.exp(similarity_scores - norm_part[:, None]).astype(jnp.bfloat16)
            return (
                acc_grad
                + jnp.dot(weights.T, question_slice_local, preferred_element_type=jnp.float32),
                None,
            )

        result, _ = lax.scan(
            per_block, running, (split_rows(q_rows, step_rows), split_rows(q_norms, step_rows))
        )
        return result

    candidate_count_overall = taken_in(
        (question_gathered_all, log_norm), ("blk", "dp"), 0, item_step, empty_grad
    )
    question_slope = direction_slope(
        (question_count_overall - candidate_gathered_all) / softmax_sharpness,
        question_direction,
        question_magnitude,
    )
    candidate_slope = direction_slope(
        (candidate_count_overall - question_gathered_all) / softmax_sharpness,
        candidate_direction,
        candidate_magnitude,
    )
    return (loss, question_slope, candidate_slope)


def solution(mesh):
    placed = (P(("blk", "dp"), None), P(("blk", "dp"), None))
    return jax.shard_map(
        per_device,
        mesh=mesh,
        in_specs=placed,
        out_specs=(P(), P(("blk", "dp"), None), P(("blk", "dp"), None)),
        check_vma=False,
    )
```

profile of v0, /device:TPU:0, one launch (start us, length us, event | category | flops | bytes accessed | tf_op | source)
XLA Modules:
  0.0 221.5 jit_solution(9734560973548897004)
XLA Ops:
  7.2 0.9 fusion.33
  8.2 1.6 fusion.37
  9.8 0.0 all-gather.6.cloned.1.call-start
  9.8 0.9 fusion.34
  10.8 1.6 fusion.38
  12.4 58.0 %all-gather.4.cloned.1.call-done = bf16[4096,256]{1,0:T(8,128)(2,1)} async-done(((bf16[128,256]{1,0:T(8,128)(2,1)}), bf16[4096,256]{1,0:T(8,128)(2,1)}) %all-gather.4.cloned.1.call-update) | async-done | bytes 2097168 | tf_op jit(solution)/shard_map/all_gather | solution.py:13
  70.4 10.8 %while.35 = (s32[]{:T(128)}, f32[128]{0:T(128)S(1)}, f32[128]{0:T(128)S(1)}, bf16[8,512,256]{2,1,0:T(8,128)(2,1)}, bf16[128,256]{1,0:T(8,128)(2,1)}, /*index=5*/s32[]{:T(128)}, s32[]{:T(128)}) while((s32[]{:T(128)}, f32[128]{0:T(128)S(1)}, f32[128]{0:T(128)S(1)}, bf16[8,512,256]{2,1,0:T(8,128)(2,1)}, bf16[128,256]{1,0:T(8,128)(2,1)}, ...), condition=%wide.region_5.0_spmd.clone, body=%wide.region_2.5_spmd.clone.sunk | while | flops 33817216 | bytes 859224 | solution.py:59
  70.4 1.2 fusion.56
  71.6 0.1 exponential_reduce_fusion.2
  71.7 1.2 fusion.56
  73.0 0.1 exponential_reduce_fusion.2
  73.1 1.2 fusion.56
  74.3 0.1 exponential_reduce_fusion.2
  74.5 1.2 fusion.56
  75.7 0.1 exponential_reduce_fusion.2
  75.8 1.2 fusion.56
  77.0 0.1 exponential_reduce_fusion.2
  77.1 1.2 fusion.56
  78.4 0.1 exponential_reduce_fusion.2
  78.5 1.2 fusion.56
  79.7 0.1 exponential_reduce_fusion.2
  79.8 1.2 fusion.56
  81.1 0.1 exponential_reduce_fusion.2
  81.2 66.5 %all-gather = f32[32,1,128]{2,1,0:T(1,128)S(1)} all-gather(f32[1,1,128]{2,1,0:T(1,128)S(1)} %bitcast.41), channel_id=1, replica_groups=mesh['blk'=2,'dp'=16] {'blk','dp'}, dimensions={0}, use_global_device_ids=true | all-gather | bytes 16896 | tf_op jit(solution)/shard_map/all_gather | solution.py:13
  147.7 0.5 broadcast.103
  148.3 0.6 reduce.5
  149.0 12.6 %while.36 = (s32[]{:T(128)}, f32[128,256]{1,0:T(8,128)S(1)}, bf16[8,512,256]{2,1,0:T(8,128)(2,1)}, bf16[128,256]{1,0:T(8,128)(2,1)}, f32[128]{0:T(128)S(1)}, /*index=5*/s32[]{:T(128)}, s32[]{:T(128)}) while((s32[]{:T(128)}, f32[128,256]{1,0:T(8,128)S(1)}, bf16[8,512,256]{2,1,0:T(8,128)(2,1)}, bf16[128,256]{1,0:T(8,128)(2,1)}, ...), condition=%wide.region_10.11_spmd.clone, body=%wide.region_9.10_spmd.clone.sunk | while | flops 67371008 | bytes 853591 | solution.py:84
  149.0 1.6 fusion.62
  150.6 1.6 fusion.62
  152.1 1.6 fusion.62
  153.7 1.6 fusion.62
  155.3 1.6 fusion.62
  156.9 1.6 fusion.62
  158.4 1.6 fusion.62
  160.0 1.6 fusion.62
  161.7 12.5 %while.37 = (s32[]{:T(128)}, f32[128,256]{1,0:T(8,128)S(1)}, bf16[8,512,256]{2,1,0:T(8,128)(2,1)}, bf16[128,256]{1,0:T(8,128)(2,1)S(1)}, f32[8,512]{1,0:T(8,128)S(1)}, /*index=5*/s32[]{:T(128)}, s32[]{:T(128)}) while((s32[]{:T(128)}, f32[128,256]{1,0:T(8,128)S(1)}, bf16[8,512,256]{2,1,0:T(8,128)(2,1)}, ...), condition=%wide.region_13.14_spmd.clone, body=%wide.region_12.13_spmd.clone.sunk | while | flops 67371008 | bytes 859227 | solution.py:111
  161.7 1.5 fusion.66
  163.3 1.5 fusion.66
  164.8 1.5 fusion.66
  166.4 1.5 fusion.66
  168.0 1.5 fusion.66
  169.5 1.5 fusion.66
  171.1 1.5 fusion.66
  172.6 1.5 fusion.66
  174.2 0.2 multiply_reduce_fusion
  174.4 0.6 subtract_reduce_fusion
  175.0 37.0 %psum.7 = f32[]{:T(128)} all-reduce(f32[]{:T(128)} %subtract_reduce_fusion), channel_id=1, replica_groups=mesh['blk'=2,'dp'=16] {'blk','dp'}, use_global_device_ids=true, to_apply=%region_8.9 | all-reduce | flops 1 | bytes 8 | tf_op jit(solution)/shard_map/psum | solution.py:67
  212.1 0.8 subtract_divide_fusion
  (50 shorter events, 0.4 us)
Async XLA Ops:
  7.2 63.2 %all-gather.4.cloned.1.call-start = ((), (), s32[]{:S(2)}) async-start(), calls=%async_computation | async-start | bytes 2162688 | tf_op jit(solution)/shard_map/all_gather | solution.py:13
  9.8 151.8 %all-gather.6.cloned.1.call-start = ((), (), s32[]{:S(2)}) async-start(), calls=%async_computation.1 | async-start | bytes 2162688 | tf_op jit(solution)/shard_map/all_gather | solution.py:13
  148.9 12.7 %copy-start = (bf16[128,256]{1,0:T(8,128)(2,1)S(1)}, bf16[128,256]{1,0:T(8,128)(2,1)}, u32[]{:S(2)}) copy-start(bf16[128,256]{1,0:T(8,128)(2,1)} %fusion.37) | copy-start | bytes 196612
  161.6 12.6 %copy-start.1 = (bf16[128,256]{1,0:T(8,128)(2,1)S(1)}, bf16[128,256]{1,0:T(8,128)(2,1)}, u32[]{:S(2)}) copy-start(bf16[128,256]{1,0:T(8,128)(2,1)} %param.9) | copy-start | bytes 196612
  161.6 12.6 %copy-start.2 = (bf16[128,256]{1,0:T(8,128)(2,1)S(1)}, bf16[128,256]{1,0:T(8,128)(2,1)}, u32[]{:S(2)}) copy-start(bf16[128,256]{1,0:T(8,128)(2,1)} %param.8) | copy-start | bytes 196612
Sparse Core Ops, SparseCore 0:
  11.4 58.9 all-gather.3
  73.8 55.2 all-gather.5
where the time goes:
time: 223 us; the launch traced here: 222 us
  blocking collectives  104 us (47%)
  waiting for transfers between devices  58 us (26%)
  matrix products  34.3 us (15%)
  between operations  16 us (7%)
  other arithmetic  8.3 us (4%)
    all_gather x1, blocking collectives, taken_in(): lax.all_gather(a, axis, axis=dim, tiled=True)  66.5 us
    all_gather x2, waiting for transfers between devices, taken_in(): lax.all_gather(a, axis, axis=dim, tiled=True)  58 us
    psum x1, blocking collectives, per_device(): loss = lax.psum(local_loss, ('blk', 'dp')) / (own_rows * devices)  37 us
    dot_general x8, matrix products, per_block(): jnp.dot(weights, candidate_slice, preferred_element_type=jnp.float32)  12.4 us
    dot_general x8, matrix products, per_block(): jnp.dot(weights.T, question_slice_local, preferred_element_type=jnp.float32)  12.2 us
    dot_general x8, matrix products, per_block(): jnp.dot(normalized_question, candidate_slice.T, preferred_element_type=jn...  9.66 us
  transfers between devices with their start and end apart: 2, of which 1 were waited for; matrix products, arithmetic and copies ran while one was open for 12% of the time, Pallas kernels for 0%

commit v1 on v0

v1 whole, which is shorter than its diff:
```python
import functools
import math

import jax
import jax.numpy as jnp
from jax import lax
from jax.experimental import pallas as pl
from jax.experimental.pallas import tpu as pltpu
from jax.sharding import PartitionSpec as P

MESH = pl.DeviceIdType.MESH

softmax_sharpness = 0.05
tiny_square = 1e-12
exponent_scale = math.log2(math.e) / softmax_sharpness


def unit_rows(matrix):
    widened = matrix.astype(jnp.float32)
    length = jnp.sqrt(jnp.sum(widened * widened, axis=1, keepdims=True) + tiny_square)
    return (widened / length, length)


def direction_slope(grad, unit, length):
    along = jnp.sum(unit * grad, axis=1, keepdims=True)
    return (grad - unit * along) / length


def folded(vector, lanes):
    pieces = [vector[:, i : i + lanes] for i in range(0, vector.shape[1], lanes)]
    return functools.reduce(jnp.add, pieces)


def kernel(
    inner,
    outer,
    cores,
    batch,
    q_hbm,
    v_hbm,
    loss_ref,
    q_out,
    v_out,
    q_raw,
    v_raw,
    q_all,
    v_all,
    weights,
    sums_all,
    totals,
    losses,
    q_part,
    v_part,
    q_in,
    v_in,
    in_sem,
    qs_send,
    qs_recv,
    vs_send,
    vs_recv,
    sum_send,
    sum_recv,
    loss_send,
    loss_recv,
    qr_send,
    qr_recv,
    vr_send,
    vr_recv,
):
    core = lax.axis_index("blk")
    spot = lax.axis_index("dp")
    across = lax.rem(spot, inner)
    along = spot // inner
    members = cores * inner
    me = core * inner + across
    rows = q_hbm.shape[0]
    f32, bf16 = jnp.float32, jnp.bfloat16

    def plane_peer(k):
        other = lax.rem(me + k, members)
        return other, (other // inner, along * inner + lax.rem(other, inner))

    def line_peer(k):
        other = lax.rem(along + k, outer)
        return other, (core, other * inner + across)

    q_load = pltpu.make_async_copy(q_hbm, q_raw, in_sem.at[0])
    v_load = pltpu.make_async_copy(v_hbm, v_raw, in_sem.at[1])
    q_load.start()
    v_load.start()
    barrier = pltpu.get_barrier_semaphore()
    for k in range(1, members):
        pl.semaphore_signal(barrier, inc=1, device_id=plane_peer(k)[1], device_id_type=MESH)
    for k in range(1, outer):
        pl.semaphore_signal(barrier, inc=1, device_id=line_peer(k)[1], device_id_type=MESH)
    v_load.wait()
    v_unit, v_len = unit_rows(v_raw[...])
    v_hat = v_unit.astype(bf16)
    v_all[along] = v_hat
    q_load.wait()
    q_unit, q_len = unit_rows(q_raw[...])
    q_hat = q_unit.astype(bf16)
    q_all[me] = q_hat
    positive = jnp.sum(q_hat.astype(f32) * v_hat.astype(f32), axis=0, keepdims=True)
    pl.semaphore_wait(barrier, members + outer - 2)

    pending = []

    def send(src, dst, send_sem, recv_sem, device):
        copy = pltpu.make_async_remote_copy(
            src_ref=src,
            dst_ref=dst,
            send_sem=send_sem,
            recv_sem=recv_sem,
            device_id=device,
            device_id_type=MESH,
        )
        copy.start()
        pending.append(copy)
        return copy

    v_moves = {}
    for k in range(outer - 1, 0, -1):
        v_moves[k] = send(
            v_all.at[along], v_all.at[along], vs_send.at[k], vs_recv.at[k], line_peer(k)[1]
        )
    q_moves = {}
    for k in range(1, members):
        q_moves[k] = send(q_all.at[me], q_all.at[me], qs_send.at[k], qs_recv.at[k], plane_peer(k)[1])

    sums_all[me] = jnp.zeros(sums_all.shape[1:], f32)
    sums_all[me, pl.ds(members, 1), :] = folded(positive, sums_all.shape[2])
    for k in range(1, outer):
        v_moves[k].wait_recv()
    v_group = v_all[...].reshape(outer * rows, v_all.shape[2])

    q_own = None
    for k in range(members):
        block = lax.rem(me + members - k, members)
        if k:
            q_moves[k].wait_recv()
        scores = lax.dot_general(
            v_group, q_all[block], (((1,), (1,)), ((), ())), preferred_element_type=f32
        )
        raised = jnp.exp2(scores * exponent_scale)
        weights[block] = raised
        sums_all[me, pl.ds(block, 1), :] = jnp.sum(raised, axis=0, keepdims=True)
    for k in range(1, members):
        send(sums_all.at[me], sums_all.at[me], sum_send.at[k], sum_recv.at[k], plane_peer(k)[1])

    q_sends = {}
    for k in list(range(1, members)) + [0]:
        block, device = plane_peer(k)
        share = lax.dot_general(
            weights[block].astype(bf16), v_group, (((0,), (0,)), ((), ())), preferred_element_type=f32
        )
        if k:
            q_part[k] = share.astype(bf16)
            q_sends[k] = send(q_part.at[k], q_in.at[k], qr_send.at[k], qr_recv.at[k], device)
        else:
            q_own = share

    for copy in pending[outer - 1 + members - 1 : outer - 1 + 2 * (members - 1)]:
        copy.wait_recv()
    message = functools.reduce(jnp.add, [sums_all[i] for i in range(members)])
    total = message[:members]
    inverse = 1.0 / total
    totals[...] = inverse
    log_norm = jnp.log(total)
    gathered_loss = jnp.sum(log_norm, axis=0, keepdims=True) - message[members : members + 1] / (
        softmax_sharpness
    )
    losses[along] = jnp.broadcast_to(gathered_loss, losses.shape[1:])

    probs = [(weights[b] * inverse[b : b + 1]).astype(bf16) for b in range(members)]
    for b in range(members):
        weights_bf = probs[b]
        q_block = q_all[b]
        part = jnp.dot(weights_bf, q_block, preferred_element_type=f32)
        if b == 0:
            v_part[...] = part
        else:
            v_part[...] += part
    v_sends = {}
    v_own = None
    v_stage = v_in.at[0]
    for k in range(outer - 1, -1, -1):
        block, device = line_peer(k)
        share = v_part[pl.ds(pl.multiple_of(block * rows, rows), rows), :]
        if k:
            v_in[outer + k] = share.astype(bf16)
            v_sends[k] = send(v_in.at[outer + k], v_in.at[k], vr_send.at[k], vr_recv.at[k], device)
        else:
            v_own = share
    loss_sends = {}
    for k in range(1, outer):
        loss_sends[k] = send(
            losses.at[along], losses.at[along], loss_send.at[k], loss_recv.at[k], line_peer(k)[1]
        )

    for k in range(1, members):
        q_sends[k].wait_recv()
        q_own = q_own + q_in[k].astype(f32)
    own_inverse = jnp.transpose(jnp.broadcast_to(totals[pl.ds(me, 1), :], (rows, rows)))[:, :1]
    q_pull = (q_own * own_inverse - v_hat.astype(f32)) / softmax_sharpness
    q_out[...] = direction_slope(q_pull, q_unit, q_len)

    for k in range(1, outer):
        loss_sends[k].wait_recv()
    loss_row = functools.reduce(jnp.add, [losses[i] for i in range(outer)])
    loss_ref[...] = jnp.broadcast_to(
        jnp.sum(loss_row[:1], axis=1, keepdims=True) / batch, loss_ref.shape
    )
    for k in range(1, outer):
        v_sends[k].wait_recv()
        v_own = v_own + v_in[k].astype(f32)
    v_pull = (v_own - q_hat.astype(f32)) / softmax_sharpness
    v_out[...] = direction_slope(v_pull, v_unit, v_len)
    for copy in pending:
        copy.wait_send()


def near_square(count):
    return max(d for d in range(1, math.isqrt(count) + 1) if count % d == 0)


def solution(mesh):
    cores, spots = mesh.shape["blk"], mesh.shape["dp"]
    outer = near_square(spots)
    inner = spots // outer
    members = cores * inner

    def per_device(queries, items):
        rows, width = queries.shape
        f32, bf16 = jnp.float32, jnp.bfloat16
        lanes = rows
        note = members + 8
        dma = pltpu.SemaphoreType.DMA
        vmem = pl.BlockSpec(memory_space=pltpu.VMEM)
        anywhere = pl.BlockSpec(memory_space=pl.ANY)
        loss, q_slope, v_slope = pl.pallas_call(
            functools.partial(kernel, inner, outer, cores, rows * cores * spots),
            out_shape=(
                jax.ShapeDtypeStruct((8, 128), f32),
                jax.ShapeDtypeStruct((rows, width), f32),
                jax.ShapeDtypeStruct((rows, width), f32),
            ),
            in_specs=[anywhere, anywhere],
            out_specs=(vmem, vmem, vmem),
            scratch_shapes=[
                pltpu.VMEM((rows, width), bf16),
                pltpu.VMEM((rows, width), bf16),
                pltpu.VMEM((members, rows, width), bf16),
                pltpu.VMEM((outer, rows, width), bf16),
                pltpu.VMEM((members, outer * rows, rows), f32),
                pltpu.VMEM((members, note, lanes), f32),
                pltpu.VMEM((members, lanes), f32),
                pltpu.VMEM((outer, 8, lanes), f32),
                pltpu.VMEM((members, rows, width), bf16),
                pltpu.VMEM((outer * rows, width), f32),
                pltpu.VMEM((members, rows, width), bf16),
                pltpu.VMEM((2 * outer, rows, width), bf16),
                dma((2,)),
                dma((members,)),
                dma((members,)),
                dma((outer,)),
                dma((outer,)),
                dma((members,)),
                dma((members,)),
                dma((outer,)),
                dma((outer,)),
                dma((members,)),
                dma((members,)),
                dma((outer,)),
                dma((outer,)),
            ],
            compiler_params=pltpu.CompilerParams(
                collective_id=0, has_side_effects=True, vmem_limit_bytes=60 * 1024 * 1024
            ),
        )(queries, items)
        return loss[0, 0], q_slope, v_slope

    placed = (P(("blk", "dp"), None), P(("blk", "dp"), None))
    return jax.shard_map(
        per_device,
        mesh=mesh,
        in_specs=placed,
        out_specs=(P(), P(("blk", "dp"), None), P(("blk", "dp"), None)),
        check_vma=False,
    )
```

time: 223 us -> 33.4 us (0.15)
  blocking collectives: 104 us -> 0 us
  waiting for transfers between devices: 58 us -> 0 us
  matrix products: 34.3 us -> 0 us
  Pallas kernels: 0 us -> 29.1 us
  between operations: 16 us -> 0.64 us
  other arithmetic: 8.3 us -> 0 us
  local copies, waits for them, and re-layouts: 0.64 us -> 3.46 us
    all_gather x1 -> x0, blocking collectives: 66.5 us -> none  [taken_in(): lax.all_gather(a, axis, axis=dim, tiled=True)]
    all_gather x2 -> x0, waiting for transfers between devices: 58 us -> none  [taken_in(): lax.all_gather(a, axis, axis=dim, tiled=True)]
    psum x1 -> x0, blocking collectives: 37 us -> none  [per_device(): loss = lax.psum(local_loss, ('blk', 'dp')) / (own_rows * devices)]
    dot_general x24 -> x0, matrix products: 34.3 us -> none  [the longest x8 12.4 us: per_block(): jnp.dot(weights, candidate_slice, preferred_element_type=jnp.float32)]
    pallas_call x0 -> x1, Pallas kernels: none -> 29.1 us  [per_device(): pl.pallas_call(functools.partial(kernel, inner, outer, cores, rows * core...]
    reduce_sum x12 -> x0, other arithmetic: 3.47 us -> none  [the longest x2 1.89 us: unit_rows(): jnp.sum(widened * widened, axis=1, keepdims=True) + tiny_square]
    convert_element_type x2 -> x0, other arithmetic: 3.14 us -> none  [the longest x1 1.57 us: per_device(): normalized_candidate = candidate_direction.astype(jnp.bfloat16)]
    unnamed x6 -> x4, local copies, waits for them, and re-layouts: 0.02 us -> 2.26 us
  transfers between devices with their start and end apart: 2 -> 0, of which waited for: 1 -> 0; matrix products, arithmetic and copies ran while one was open for 12% -> 0% of each run, Pallas kernels for 0% -> 0%
where the time goes in v1:
time: 33.4 us; the launch traced here: 33.2 us
  Pallas kernels  29.1 us (87%)
  local copies, waits for them, and re-layouts  3.46 us (10%)
  between operations  0.64 us (2%)
    pallas_call x1, Pallas kernels, per_device(): pl.pallas_call(functools.partial(kernel, inner, outer, cores, rows * core...  29.1 us
    unnamed x4, local copies, waits for them, and re-layouts  2.26 us
    slice x1, local copies, waits for them, and re-layouts, per_device(): return (loss[0, 0], q_slope, v_slope)  1.19 us

profile of v1, /device:TPU:0, one launch (start us, length us, event | category | flops | bytes accessed | tf_op | source)
XLA Modules:
  0.0 33.2 jit_solution(1718402086193679584)
XLA Ops:
  0.6 29.1 %shard_map.49 = (f32[8,128]{1,0:T(8,128)}, f32[128,256]{1,0:T(8,128)}, f32[128,256]{1,0:T(8,128)}) custom-call(bf16[128,256]{1,0:T(8,128)(2,1)} %q_hbm.1, bf16[128,256]{1,0:T(8,128)(2,1)} %v_hbm.1), custom_call_target="tpu_custom_call" | custom-call | tf_op jit(solution)/shard_map/pallas_call | solution.py:241
  29.8 1.2 %slice.3 = f32[1,1]{1,0:T(1,128)} slice(f32[8,128]{1,0:T(8,128)} %get-tuple-element.6), slice={[0:1], [0:1]} | slice | bytes 8 | tf_op jit(solution)/shard_map/slice | solution.py:281
  30.9 0.0 copy-start
  30.9 1.6 %copy.7 = f32[128,256]{1,0:T(8,128)} copy(f32[128,256]{1,0:T(8,128)} %get-tuple-element.13) | data formatting | bytes 262144
  32.5 0.0 copy-done
  32.6 0.7 %copy.8 = f32[128,256]{1,0:T(8,128)} copy(f32[128,256]{1,0:T(8,128)S(1)} %copy-done) | data formatting | bytes 262144
Async XLA Ops:
  30.9 1.6 %copy-start = (f32[128,256]{1,0:T(8,128)S(1)}, f32[128,256]{1,0:T(8,128)}, u32[]{:S(2)}) copy-start(f32[128,256]{1,0:T(8,128)} %get-tuple-element.14) | copy-start | bytes 393220

commit v2 on v1

v2 whole, which is shorter than its diff:
```python
import functools
import math

import jax
import jax.numpy as jnp
from jax import lax
from jax.experimental import pallas as pl
from jax.experimental.pallas import tpu as pltpu
from jax.sharding import PartitionSpec as P

MESH = pl.DeviceIdType.MESH

softmax_sharpness = 0.05
tiny_square = 1e-12
exponent_scale = math.log2(math.e) / softmax_sharpness


def unit_rows(matrix):
    widened = matrix.astype(jnp.float32)
    length = jnp.sqrt(jnp.sum(widened * widened, axis=1, keepdims=True) + tiny_square)
    return (widened / length, length)


def direction_slope(grad, unit, length):
    along = jnp.sum(unit * grad, axis=1, keepdims=True)
    return (grad - unit * along) / length


def folded(vector, lanes):
    pieces = [vector[:, i : i + lanes] for i in range(0, vector.shape[1], lanes)]
    return functools.reduce(jnp.add, pieces)


def partner(spot, step, count):
    if count & (count - 1):
        return lax.rem(spot + step, count)
    other = spot
    bit = 1
    while bit < count:
        if step & bit:
            other = other + bit * (1 - 2 * lax.rem(spot // bit, 2))
        bit *= 2
    return other


def source(spot, step, count):
    if count & (count - 1):
        return lax.rem(spot + count - step, count)
    return partner(spot, step, count)


def kernel(
    inner,
    outer,
    cores,
    q_hbm,
    v_hbm,
    loss_ref,
    q_out,
    v_out,
    q_raw,
    v_raw,
    q_all,
    v_all,
    weights,
    q_sum,
    sums_all,
    totals,
    losses,
    q_part,
    v_part,
    q_in,
    v_in,
    in_sem,
    qs_send,
    qs_recv,
    qf_send,
    qf_recv,
    vs_send,
    vs_recv,
    sum_send,
    sum_recv,
    loss_send,
    loss_recv,
    qr_send,
    qr_recv,
    vr_send,
    vr_recv,
):
    core = lax.axis_index("blk")
    spot = lax.axis_index("dp")
    across = lax.rem(spot, inner)
    along = spot // inner
    members = cores * inner
    me = core * inner + across
    rows = q_hbm.shape[0]
    width = q_hbm.shape[1]
    batch = rows * members * outer
    f32, bf16 = jnp.float32, jnp.bfloat16
    plane_steps = [(c, s) for s in range(inner) for c in range(cores) if c or s]
    line_steps = list(range(outer - 1, 0, -1))

    def plane_peer(step):
        c, s = step
        there_core, there = partner(core, c, cores), partner(across, s, inner)
        return there_core * inner + there, (there_core, along * inner + there)

    def plane_source(step):
        c, s = step
        return source(core, c, cores) * inner + source(across, s, inner)

    def line_peer(s):
        there = partner(along, s, outer)
        return there, (core, there * inner + across)

    def plane_key(step):
        return step[1] * cores + step[0]

    q_load = pltpu.make_async_copy(q_hbm, q_raw, in_sem.at[0])
    v_load = pltpu.make_async_copy(v_hbm, v_raw, in_sem.at[1])
    v_load.start()
    q_load.start()
    barrier = pltpu.get_barrier_semaphore()
    for s in line_steps:
        pl.semaphore_signal(barrier, inc=1, device_id=line_peer(s)[1], device_id_type=MESH)
    for step in plane_steps:
        pl.semaphore_signal(barrier, inc=1, device_id=plane_peer(step)[1], device_id_type=MESH)
    v_load.wait()
    v_unit, v_len = unit_rows(v_raw[...])
    v_hat = v_unit.astype(bf16)
    v_all[along] = v_hat
    q_load.wait()
    q_unit, q_len = unit_rows(q_raw[...])
    q_hat = q_unit.astype(bf16)
    q_all[me] = q_hat
    positive = jnp.sum(q_hat.astype(f32) * v_hat.astype(f32), axis=0, keepdims=True)
    pl.semaphore_wait(barrier, members + outer - 2)

    pending = []

    def send(src, dst, send_sem, recv_sem, device):
        copy = pltpu.make_async_remote_copy(
            src_ref=src,
            dst_ref=dst,
            send_sem=send_sem,
            recv_sem=recv_sem,
            device_id=device,
            device_id_type=MESH,
        )
        copy.start()
        pending.append(copy)
        return copy

    v_moves = {}
    for s in line_steps:
        v_moves[s] = send(
            v_all.at[along], v_all.at[along], vs_send.at[s], vs_recv.at[s], line_peer(s)[1]
        )
    q_moves = {}
    for s in range(inner - 1, 0, -1):
        q_moves[s] = send(
            q_all.at[me], q_all.at[me], qs_send.at[s], qs_recv.at[s], plane_peer((0, s))[1]
        )
    forwards = []

    def pass_on(s):
        slot = plane_source((0, s))
        for c in range(1, cores):
            key = plane_key((c, s))
            there = plane_peer((c, 0))[1]
            forwards.append(
                send(q_all.at[slot], q_all.at[slot], qf_send.at[key], qf_recv.at[key], there)
            )

    pass_on(0)
    sums_all[me] = jnp.zeros(sums_all.shape[1:], f32)
    sums_all[me, pl.ds(members, 1), :] = folded(positive, sums_all.shape[2])
    for s in range(1, inner):
        q_moves[s].wait_recv()
        pass_on(s)
    for copy in forwards:
        copy.wait_recv()
    q_group = q_all[...].reshape(members * rows, width)

    summed = None
    for n, s in enumerate([0] + line_steps[::-1]):
        if s:
            v_moves[s].wait_recv()
        slot = source(along, s, outer) if s else along
        v_block = v_all[slot]
        scores = lax.dot_general(
            v_block, q_group, (((1,), (1,)), ((), ())), preferred_element_type=f32
        )
        raised = jnp.exp2(scores * exponent_scale)
        weights[slot] = raised
        below = jnp.sum(raised, axis=0, keepdims=True)
        summed = below if summed is None else summed + below
        if n == outer - 1:
            for b in range(members):
                sums_all[me, pl.ds(b, 1), :] = summed[:, b * rows : (b + 1) * rows]
            sum_moves = {}
            for step in plane_steps:
                key = plane_key(step)
                sum_moves[step] = send(
                    sums_all.at[me],
                    sums_all.at[me],
                    sum_send.at[key],
                    sum_recv.at[key],
                    plane_peer(step)[1],
                )
        share = lax.dot_general(
            raised.astype(bf16), v_block, (((0,), (0,)), ((), ())), preferred_element_type=f32
        ).reshape(members, rows, width)
        if n == 0:
            q_sum[...] = share
        elif n < outer - 1:
            q_sum[...] += share
        else:
            q_sum[...] += share

    q_moves = {}
    for step in plane_steps[::-1]:
        key = plane_key(step)
        there, device = plane_peer(step)
        q_part[key] = q_sum[there].astype(bf16)
        q_moves[step] = send(q_part.at[key], q_in.at[key], qr_send.at[key], qr_recv.at[key], device)

    for step in plane_steps:
        sum_moves[step].wait_recv()
    message = functools.reduce(jnp.add, [sums_all[i] for i in range(members)])
    total = message[:members]
    inverse = 1.0 / total
    totals[...] = inverse
    inverse_row = jnp.concatenate([inverse[b : b + 1] for b in range(members)], axis=1)
    v_moves = {}
    for s in line_steps + [0]:
        slot, device = line_peer(s)
        probs = (weights[slot] * inverse_row).astype(bf16)
        share = jnp.dot(probs, q_group, preferred_element_type=f32)
        if s:
            v_part[s] = share.astype(bf16)
            v_moves[s] = send(v_part.at[s], v_in.at[s], vr_send.at[s], vr_recv.at[s], device)
        else:
            v_own = share
    log_norm = jnp.log(total)
    gathered_loss = (
        jnp.sum(log_norm, axis=0, keepdims=True)
        - message[members : members + 1] / softmax_sharpness
    )
    losses[along] = jnp.broadcast_to(gathered_loss, losses.shape[1:])
    loss_moves = {}
    for s in line_steps:
        loss_moves[s] = send(
            losses.at[along], losses.at[along], loss_send.at[s], loss_recv.at[s], line_peer(s)[1]
        )

    q_own = q_sum[me]
    for step in plane_steps:
        q_moves[step].wait_recv()
        q_own = q_own + q_in[plane_key(step)].astype(f32)
    own_inverse = jnp.transpose(jnp.broadcast_to(totals[pl.ds(me, 1), :], (rows, rows)))[:, :1]
    q_pull = (q_own * own_inverse - v_all[along].astype(f32)) / softmax_sharpness
    q_unit, q_len = unit_rows(q_raw[...])
    q_out[...] = direction_slope(q_pull, q_unit, q_len)

    for s in line_steps[::-1]:
        v_moves[s].wait_recv()
        v_own = v_own + v_in[s].astype(f32)
    v_pull = (v_own - q_all[me].astype(f32)) / softmax_sharpness
    v_unit, v_len = unit_rows(v_raw[...])
    v_out[...] = direction_slope(v_pull, v_unit, v_len)
    for s in line_steps:
        loss_moves[s].wait_recv()
    loss_row = functools.reduce(jnp.add, [losses[i] for i in range(outer)])
    loss_ref[0, 0] = jnp.sum(loss_row[:1]) / batch
    for copy in pending:
        copy.wait_send()


def near_square(count):
    return max(d for d in range(1, math.isqrt(count) + 1) if count % d == 0)


def solution(mesh):
    cores, spots = mesh.shape["blk"], mesh.shape["dp"]
    outer = near_square(spots)
    inner = spots // outer
    members = cores * inner

    def per_device(queries, items):
        rows, width = queries.shape
        f32, bf16 = jnp.float32, jnp.bfloat16
        lanes = rows
        note = members + 8
        dma = pltpu.SemaphoreType.DMA
        vmem = pl.BlockSpec(memory_space=pltpu.VMEM)
        anywhere = pl.BlockSpec(memory_space=pl.ANY)
        loss, q_slope, v_slope = pl.pallas_call(
            functools.partial(kernel, inner, outer, cores),
            out_shape=(
                jax.ShapeDtypeStruct((1, 1), f32),
                jax.ShapeDtypeStruct((rows, width), f32),
                jax.ShapeDtypeStruct((rows, width), f32),
            ),
            in_specs=[anywhere, anywhere],
            out_specs=(pl.BlockSpec(memory_space=pltpu.SMEM), vmem, vmem),
            scratch_shapes=[
                pltpu.VMEM((rows, width), bf16),
                pltpu.VMEM((rows, width), bf16),
                pltpu.VMEM((members, rows, width), bf16),
                pltpu.VMEM((outer, rows, width), bf16),
                pltpu.VMEM((outer, rows, members * rows), f32),
                pltpu.VMEM((members, rows, width), f32),
                pltpu.VMEM((members, note, lanes), f32),
                pltpu.VMEM((members, lanes), f32),
                pltpu.VMEM((outer, 8, lanes), f32),
                pltpu.VMEM((members, rows, width), bf16),
                pltpu.VMEM((outer, rows, width), bf16),
                pltpu.VMEM((members, rows, width), bf16),
                pltpu.VMEM((outer, rows, width), bf16),
                dma((2,)),
                dma((inner,)),
                dma((inner,)),
                dma((members,)),
                dma((members,)),
                dma((outer,)),
                dma((outer,)),
                dma((members,)),
                dma((members,)),
                dma((outer,)),
                dma((outer,)),
                dma((members,)),
                dma((members,)),
                dma((outer,)),
                dma((outer,)),
            ],
            compiler_params=pltpu.CompilerParams(
                collective_id=0, has_side_effects=True, vmem_limit_bytes=60 * 1024 * 1024
            ),
        )(queries, items)
        return loss.reshape(()), q_slope, v_slope

    placed = (P(("blk", "dp"), None), P(("blk", "dp"), None))
    return jax.shard_map(
        per_device,
        mesh=mesh,
        in_specs=placed,
        out_specs=(P(), P(("blk", "dp"), None), P(("blk", "dp"), None)),
        check_vma=False,
    )
```

time: 33.4 us -> 31.6 us (0.946)
  Pallas kernels: 29.1 us -> 26.8 us
  between operations: 0.64 us -> 2.32 us
  local copies, waits for them, and re-layouts: 3.46 us -> 2.26 us
    pallas_call x1, Pallas kernels: 29.1 us -> 26.8 us  [per_device(): pl.pallas_call(functools.partial(kernel, inner, outer, cores), out_shape=...]
    slice x1 -> x0, local copies, waits for them, and re-layouts: 1.19 us -> none  [per_device(): return (loss[0, 0], q_slope, v_slope)]
where the time goes in v2:
time: 31.6 us; the launch traced here: 31.4 us
  Pallas kernels  26.8 us (85%)
  between operations  2.32 us (7%)
  local copies, waits for them, and re-layouts  2.26 us (7%)
    pallas_call x1, Pallas kernels, per_device(): pl.pallas_call(functools.partial(kernel, inner, outer, cores), out_shape=...  26.8 us
    unnamed x4, local copies, waits for them, and re-layouts  2.26 us

profile of v2, /device:TPU:0, one launch (start us, length us, event | category | flops | bytes accessed | tf_op | source)
XLA Modules:
  0.0 31.4 jit_solution(206203285087459113)
XLA Ops:
  0.6 26.8 %shard_map.49 = (f32[1,1]{1,0:T(1,128)}, f32[128,256]{1,0:T(8,128)}, f32[128,256]{1,0:T(8,128)}) custom-call(bf16[128,256]{1,0:T(8,128)(2,1)} %q_hbm.1, bf16[128,256]{1,0:T(8,128)(2,1)} %v_hbm.1), custom_call_target="tpu_custom_call" | custom-call | tf_op jit(solution)/shard_map/pallas_call | solution.py:298
  28.0 0.0 copy-start
  28.0 1.6 %copy.9 = f32[128,256]{1,0:T(8,128)} copy(f32[128,256]{1,0:T(8,128)} %get-tuple-element.13) | data formatting | bytes 262144
  29.6 0.0 copy-done
  29.6 0.7 %copy.10 = f32[128,256]{1,0:T(8,128)} copy(f32[128,256]{1,0:T(8,128)S(1)} %copy-done) | data formatting | bytes 262144
Async XLA Ops:
  28.0 1.6 %copy-start = (f32[128,256]{1,0:T(8,128)S(1)}, f32[128,256]{1,0:T(8,128)}, u32[]{:S(2)}) copy-start(f32[128,256]{1,0:T(8,128)} %get-tuple-element.14) | copy-start | bytes 393220

commit v3 on v2

--- a/solution.py
+++ b/solution.py
@@ -259,14 +259,14 @@
         q_moves[step].wait_recv()
         q_own = q_own + q_in[plane_key(step)].astype(f32)
     own_inverse = jnp.transpose(jnp.broadcast_to(totals[pl.ds(me, 1), :], (rows, rows)))[:, :1]
-    q_pull = (q_own * own_inverse - v_all[along].astype(f32)) / softmax_sharpness
+    q_pull = (q_own * own_inverse - v_all[along].astype(f32))
     q_unit, q_len = unit_rows(q_raw[...])
     q_out[...] = direction_slope(q_pull, q_unit, q_len)
 
     for s in line_steps[::-1]:
         v_moves[s].wait_recv()
         v_own = v_own + v_in[s].astype(f32)
-    v_pull = (v_own - q_all[me].astype(f32)) / softmax_sharpness
+    v_pull = (v_own - q_all[me].astype(f32))
     v_unit, v_len = unit_rows(v_raw[...])
     v_out[...] = direction_slope(v_pull, v_unit, v_len)
     for s in line_steps:
@@ -299,8 +299,8 @@
             functools.partial(kernel, inner, outer, cores),
             out_shape=(
                 jax.ShapeDtypeStruct((1, 1), f32),
-                jax.ShapeDtypeStruct((rows, width), f32),
-                jax.ShapeDtypeStruct((rows, width), f32),
+                pltpu.VMEM((rows, width), f32),
+                pltpu.VMEM((rows, width), f32),
             ),
             in_specs=[anywhere, anywhere],
             out_specs=(pl.BlockSpec(memory_space=pltpu.SMEM), vmem, vmem),
@@ -338,7 +338,7 @@
                 collective_id=0, has_side_effects=True, vmem_limit_bytes=60 * 1024 * 1024
             ),
         )(queries, items)
-        return loss.reshape(()), q_slope, v_slope
+        return loss.reshape(()), q_slope / softmax_sharpness, v_slope / softmax_sharpness
 
     placed = (P(("blk", "dp"), None), P(("blk", "dp"), None))
     return jax.shard_map(

time: 31.6 us -> 30 us (0.949)
  local copies, waits for them, and re-layouts: 2.26 us -> 0 us
  other arithmetic: 0 us -> 0.72 us
    unnamed x4 -> x0, local copies, waits for them, and re-layouts: 2.26 us -> none
    div x0 -> x1, other arithmetic: none -> 0.72 us  [per_device(): v_slope / softmax_sharpness]
where the time goes in v3:
time: 30 us; the launch traced here: 29.8 us
  Pallas kernels  26.6 us (89%)
  between operations  2.4 us (8%)
  other arithmetic  0.72 us (2%)
    pallas_call x1, Pallas kernels, per_device(): pl.pallas_call(functools.partial(kernel, inner, outer, cores), out_shape=...  26.6 us
    div x1, other arithmetic, per_device(): v_slope / softmax_sharpness  0.72 us

profile of v3, /device:TPU:0, one launch (start us, length us, event | category | flops | bytes accessed | tf_op | source)
XLA Modules:
  0.0 29.8 jit_solution(17125197223090446936)
XLA Ops:
  0.6 26.6 %shard_map.49 = (f32[1,1]{1,0:T(1,128)}, f32[128,256]{1,0:T(8,128)S(1)}, f32[128,256]{1,0:T(8,128)S(1)}) custom-call(bf16[128,256]{1,0:T(8,128)(2,1)} %q_hbm.1, bf16[128,256]{1,0:T(8,128)(2,1)} %v_hbm.1), custom_call_target="tpu_custom_call" | custom-call | tf_op jit(solution)/shard_map/pallas_call | solution.py:298
  27.3 0.7 %broadcast_multiply_fusion = (f32[128,256]{1,0:T(8,128)}, f32[128,256]{1,0:T(8,128)}) fusion(f32[128,256]{1,0:T(8,128)S(1)} %get-tuple-element.8, f32[128,256]{1,0:T(8,128)S(1)} %get-tuple-element.7), kind=kLoop, calls=%fused_computation | loop fusion | flops 65536 | bytes 524288 | tf_op jit(solution)/shard_map/div | solution.py:341

commit v4 on v3

--- a/solution.py
+++ b/solution.py
@@ -71,6 +71,9 @@
     v_part,
     q_in,
     v_in,
+    v_sum,
+    units,
+    shrink,
     in_sem,
     qs_send,
     qs_recv,
@@ -99,6 +102,7 @@
     f32, bf16 = jnp.float32, jnp.bfloat16
     plane_steps = [(c, s) for s in range(inner) for c in range(cores) if c or s]
     line_steps = list(range(outer - 1, 0, -1))
+    arrivals = [s for s in line_steps[::-1] if s != 2] + [s for s in line_steps if s == 2]
 
     def plane_peer(step):
         c, s = step
@@ -183,7 +187,7 @@
     q_group = q_all[...].reshape(members * rows, width)
 
     summed = None
-    for n, s in enumerate([0] + line_steps[::-1]):
+    for n, s in enumerate([0] + arrivals):
         if s:
             v_moves[s].wait_recv()
         slot = source(along, s, outer) if s else along
@@ -231,6 +235,17 @@
     total = message[:members]
     inverse = 1.0 / total
     totals[...] = inverse
+    log_norm = jnp.log(total)
+    gathered_loss = (
+        jnp.sum(log_norm, axis=0, keepdims=True)
+        - message[members : members + 1] / softmax_sharpness
+    )
+    losses[along] = jnp.broadcast_to(gathered_loss, losses.shape[1:])
+    loss_moves = {}
+    for s in line_steps:
+        loss_moves[s] = send(
+            losses.at[along], losses.at[along], loss_send.at[s], loss_recv.at[s], line_peer(s)[1]
+        )
     inverse_row = jnp.concatenate([inverse[b : b + 1] for b in range(members)], axis=1)
     v_moves = {}
     for s in line_steps + [0]:
@@ -242,18 +257,6 @@
             v_moves[s] = send(v_part.at[s], v_in.at[s], vr_send.at[s], vr_recv.at[s], device)
         else:
             v_own = share
-    log_norm = jnp.log(total)
-    gathered_loss = (
-        jnp.sum(log_norm, axis=0, keepdims=True)
-        - message[members : members + 1] / softmax_sharpness
-    )
-    losses[along] = jnp.broadcast_to(gathered_loss, losses.shape[1:])
-    loss_moves = {}
-    for s in line_steps:
-        loss_moves[s] = send(
-            losses.at[along], losses.at[along], loss_send.at[s], loss_recv.at[s], line_peer(s)[1]
-        )
-
     q_own = q_sum[me]
     for step in plane_steps:
         q_moves[step].wait_recv()
@@ -263,16 +266,23 @@
     q_unit, q_len = unit_rows(q_raw[...])
     q_out[...] = direction_slope(q_pull, q_unit, q_len)
 
-    for s in line_steps[::-1]:
-        v_moves[s].wait_recv()
-        v_own = v_own + v_in[s].astype(f32)
-    v_pull = (v_own - q_all[me].astype(f32))
     v_unit, v_len = unit_rows(v_raw[...])
-    v_out[...] = direction_slope(v_pull, v_unit, v_len)
+    units[...] = v_unit
+    shrink[...] = jnp.broadcast_to(1.0 / v_len, shrink.shape)
+    v_sum[...] = v_own - q_all[me].astype(f32)
     for s in line_steps:
         loss_moves[s].wait_recv()
     loss_row = functools.reduce(jnp.add, [losses[i] for i in range(outer)])
     loss_ref[0, 0] = jnp.sum(loss_row[:1]) / batch
+    for s in arrivals[:-1]:
+        v_moves[s].wait_recv()
+        v_sum[...] += v_in[s].astype(f32)
+    for s in arrivals[-1:]:
+        v_moves[s].wait_recv()
+    v_pull = v_sum[...] + v_in[arrivals[-1]].astype(f32)
+    v_unit = units[...]
+    along_unit = jnp.sum(v_unit * v_pull, axis=1, keepdims=True)
+    v_out[...] = (v_pull - v_unit * along_unit) * shrink[...]
     for copy in pending:
         copy.wait_send()
 
@@ -318,6 +328,9 @@
                 pltpu.VMEM((outer, rows, width), bf16),
                 pltpu.VMEM((members, rows, width), bf16),
                 pltpu.VMEM((outer, rows, width), bf16),
+                pltpu.VMEM((rows, width), f32),
+                pltpu.VMEM((rows, width), f32),
+                pltpu.VMEM((rows, width), f32),
                 dma((2,)),
                 dma((inner,)),
                 dma((inner,)),

time: 30 us -> 29.5 us (0.983)
  Pallas kernels: 26.6 us -> 26.1 us
    pallas_call x1, Pallas kernels: 26.6 us -> 26.1 us  [per_device(): pl.pallas_call(functools.partial(kernel, inner, outer, cores), out_shape=...]
where the time goes in v4:
time: 29.5 us; the launch traced here: 29.2 us
  Pallas kernels  26.1 us (88%)
  between operations  2.4 us (8%)
  other arithmetic  0.72 us (2%)
    pallas_call x1, Pallas kernels, per_device(): pl.pallas_call(functools.partial(kernel, inner, outer, cores), out_shape=...  26.1 us
    div x1, other arithmetic, per_device(): v_slope / softmax_sharpness  0.72 us

profile of v4, /device:TPU:0, one launch (start us, length us, event | category | flops | bytes accessed | tf_op | source)
XLA Modules:
  0.0 29.2 jit_solution(10074202153801950953)
XLA Ops:
  0.6 26.1 %shard_map.49 = (f32[1,1]{1,0:T(1,128)}, f32[128,256]{1,0:T(8,128)S(1)}, f32[128,256]{1,0:T(8,128)S(1)}) custom-call(bf16[128,256]{1,0:T(8,128)(2,1)} %q_hbm.1, bf16[128,256]{1,0:T(8,128)(2,1)} %v_hbm.1), custom_call_target="tpu_custom_call" | custom-call | tf_op jit(solution)/shard_map/pallas_call | solution.py:308
  26.8 0.7 %broadcast_multiply_fusion = (f32[128,256]{1,0:T(8,128)}, f32[128,256]{1,0:T(8,128)}) fusion(f32[128,256]{1,0:T(8,128)S(1)} %get-tuple-element.8, f32[128,256]{1,0:T(8,128)S(1)} %get-tuple-element.7), kind=kLoop, calls=%fused_computation | loop fusion | flops 65536 | bytes 524288 | tf_op jit(solution)/shard_map/div | solution.py:354
